TPU v7x, 32 devices: a whole 2x2x4 slice. The times are simulated.
32 devices in a mesh: seq: 4 (over z), tensor: 2 (over x), dp: 4 (over y, core).
Axes of the slice: x: 2, y: 2, z: 4, core: 2. Of those that a mesh axis runs over, the one named last changes fastest.
Arguments:
- tokens: bfloat16 [4, 1024, 3072], P('dp', 'seq'), may hold values from -6 to 6
- cotangent: bfloat16 [4, 1024, 3072], P('dp', 'seq'), may hold values from -6 to 6
- qkv_weight: bfloat16 [3072, 3, 768], P(('seq', 'dp'), None, 'tensor'), may hold values from -0.109375 to 0.109375
- out_weight: bfloat16 [3072, 768], P(('seq', 'dp'), 'tensor'), may hold values from -0.21875 to 0.21875
Outputs:
- qkv_grad: float32 [3072, 3, 768], P(('seq', 'dp'), None, 'tensor')
- out_grad: float32 [3072, 768], P(('seq', 'dp'), 'tensor')
- branch_grad: bfloat16 [4, 1024, 3072], P('dp', 'seq', 'tensor')
All inputs are finite; a program needn't handle non-finite values.
Results may differ from a plain program's by a relative error of at most 0.025.
Values may be sent and summed in bfloat16 or wider, within the bound.
A program may use at most 128 MiB of HBM per device.

v0:
```python
import jax
import jax.numpy as jnp
from jax import lax
from jax.sharding import PartitionSpec as P

HD = 128
epsilon = 1e-06


def normalize(values):
    average = jnp.mean(values, axis=-1, keepdims=True)
    centered = values - average
    inverse = lax.rsqrt(jnp.mean(centered * centered, axis=-1, keepdims=True) + epsilon)
    return (centered * inverse, inverse)


def normalize_back(gradient, normed, inverse):
    mean_grad = jnp.mean(gradient, axis=-1, keepdims=True)
    mean_both = jnp.mean(gradient * normed, axis=-1, keepdims=True)
    return (gradient - mean_grad - normed * mean_both) * inverse


def local(tokens, cotangent, qkv_weight, out_weight):
    row_count = tokens.shape[1]
    feature_count = tokens.shape[2]
    column_count = out_weight.shape[1]
    head_count = column_count // HD
    score_scale = HD ** (-0.5)
    own_rows = qkv_weight.shape[0]
    grad_rows = cotangent[0]
    normed, inverse = normalize(tokens[0].astype(jnp.float32))
    unit_low = normed.astype(jnp.bfloat16)
    flat_weight = qkv_weight.reshape(own_rows, 3 * column_count)
    piece_qkv = lax.all_gather(flat_weight, ("seq", "dp"), axis=0, tiled=True)
    piece_out = lax.all_gather(out_weight, ("seq", "dp"), axis=0, tiled=True)
    piece_rows = piece_qkv.shape[0]
    left_rows = unit_low
    right_rows = grad_rows
    projected = jnp.dot(left_rows, piece_qkv, preferred_element_type=jnp.float32)
    attended_grad = jnp.dot(right_rows, piece_out, preferred_element_type=jnp.float32)
    full_qkv = piece_qkv
    projected, attended_grad, full_qkv = (projected, attended_grad, full_qkv)
    query_unit, query_inv = normalize(
        projected[:, :column_count].reshape(row_count, head_count, HD)
    )
    key_unit, key_inv = normalize(
        projected[:, column_count : 2 * column_count].reshape(row_count, head_count, HD)
    )
    query_low = query_unit.astype(jnp.bfloat16)
    key_value = jnp.stack(
        [
            key_unit.astype(jnp.bfloat16).reshape(row_count, column_count),
            projected[:, 2 * column_count :].astype(jnp.bfloat16),
        ]
    )
    grad_low = attended_grad.astype(jnp.bfloat16).reshape(row_count, head_count, HD)

    def scores_of(key_rows):
        piece_rows = key_rows.shape[0]
        return (
            jnp.einsum(
                "qhd,khd->hqk",
                query_low,
                key_rows.reshape(piece_rows, head_count, HD),
                preferred_element_type=jnp.float32,
            )
            * score_scale
        )

    every_pair = lax.all_gather(key_value, "seq", axis=1, tiled=True)
    piece_rows = every_pair.shape[1]
    exponent = jnp.exp(scores_of(every_pair[0]))
    add_exp_total = jnp.sum(exponent, axis=-1)
    weighted = jnp.einsum(
        "hqk,khd->qhd",
        exponent.astype(jnp.bfloat16),
        every_pair[1].reshape(piece_rows, head_count, HD),
        preferred_element_type=jnp.float32,
    )
    exp_total, weighted = (add_exp_total, weighted)
    attended_low = (weighted / exp_total.T[:, :, None]).astype(jnp.bfloat16)
    row_delta = jnp.sum(grad_low.astype(jnp.float32) * attended_low.astype(jnp.float32), axis=-1)
    piece_rows = every_pair.shape[1]
    key_rows = every_pair[0].reshape(piece_rows, head_count, HD)
    value_rows = every_pair[1].reshape(piece_rows, head_count, HD)
    probability = jnp.exp(scores_of(every_pair[0])) / exp_total[:, :, None]
    prob_grad = jnp.einsum("qhd,khd->hqk", grad_low, value_rows, preferred_element_type=jnp.float32)
    grad_score = (probability * (prob_grad - row_delta.T[:, :, None]) * score_scale).astype(
        jnp.bfloat16
    )
    query_part = jnp.einsum(
        "hqk,khd->qhd", grad_score, key_rows, preferred_element_type=jnp.float32
    )
    key_part = jnp.einsum("hqk,qhd->khd", grad_score, query_low, preferred_element_type=jnp.float32)
    value_part = jnp.einsum(
        "hqk,qhd->khd",
        probability.astype(jnp.bfloat16),
        grad_low,
        preferred_element_type=jnp.float32,
    )
    every_grad = jnp.stack(
        [key_part.reshape(piece_rows, column_count), value_part.reshape(piece_rows, column_count)]
    )
    pair_grad = lax.psum_scatter(
        every_grad.astype(jnp.bfloat16), "seq", scatter_dimension=1, tiled=True
    ).astype(jnp.float32)
    query_back = normalize_back(query_part, query_unit, query_inv)
    key_back = normalize_back(pair_grad[0].reshape(row_count, head_count, HD), key_unit, key_inv)
    qkv_low = jnp.concatenate(
        [
            query_back.reshape(row_count, column_count),
            key_back.reshape(row_count, column_count),
            pair_grad[1],
        ],
        axis=1,
    ).astype(jnp.bfloat16)
    inner_grad = jnp.einsum("rc,dc->rd", qkv_low, full_qkv, preferred_element_type=jnp.float32)
    attended_flat = attended_low.reshape(row_count, column_count)
    share_width = feature_count // lax.axis_size("tensor")
    whole_sum = lax.psum(inner_grad.astype(jnp.bfloat16), "tensor").astype(jnp.float32)
    branch = lax.dynamic_slice_in_dim(
        normalize_back(whole_sum, normed, inverse),
        lax.axis_index("tensor") * share_width,
        share_width,
        1,
    )
    left_rows = unit_low
    right_rows = grad_rows
    qkv_term = jnp.einsum(
        "rd,rc->dc", left_rows, qkv_low, preferred_element_type=jnp.float32
    ).reshape(lax.axis_size(("seq", "dp")) * own_rows, 3, column_count)
    out_term = jnp.einsum(
        "rd,rc->dc", right_rows, attended_flat, preferred_element_type=jnp.float32
    )
    summed = lax.psum_scatter(
        jnp.concatenate([qkv_term, out_term[:, None, :]], axis=1).astype(jnp.bfloat16),
        ("seq", "dp"),
        scatter_dimension=0,
        tiled=True,
    ).astype(jnp.float32)
    return (summed[:, :3], summed[:, 3], branch.astype(jnp.bfloat16)[None])


def solution(mesh):
    return jax.shard_map(
        local,
        mesh=mesh,
        in_specs=(
            P("dp", "seq", None),
            P("dp", "seq", None),
            P(("seq", "dp"), None, "tensor"),
            P(("seq", "dp"), "tensor"),
        ),
        out_specs=(
            P(("seq", "dp"), None, "tensor"),
            P(("seq", "dp"), "tensor"),
            P("dp", "seq", "tensor"),
        ),
        check_vma=False,
    )
```

profile of v0, /device:TPU:0, one launch (start us, length us, event | category | flops | bytes accessed | tf_op | source)
XLA Modules:
  0.0 413.4 jit_solution(1419548005790425770)
XLA Ops:
  7.2 2.0 copy.55
  9.3 0.7 all-gather.8.cloned.1.call-update
  10.0 1.7 convert_reduce_fusion
  11.8 0.6 fusion.6
  12.3 67.3 %all-gather.4.cloned.1.call-done = bf16[3072,1152]{1,0:T(8,128)(2,1)} async-done(((bf16[192,1152]{1,0:T(8,128)(2,1)}), bf16[3072,1152]{1,0:T(8,128)(2,1)}) %all-gather.4.cloned.1.call-update) | async-done | bytes 7077904 | tf_op jit(solution)/shard_map/all_gather | solution.py:34
  79.6 5.3 %fusion.23 = f32[256,1152]{1,0:T(8,128)S(1)} fusion(bf16[3072,1152]{1,0:T(8,128)(2,1)} %all-gather.4.cloned.1.call-done, bf16[1,256,3072]{2,1,0:T(8,128)(2,1)S(1)} %copy-done.1, f32[256]{0:T(256)S(1)} %add_rsqrt_fusion.2, f32[256]{0:T(256)S(1)} %broadcast_multiply_fusion.8), kind=kOutput, calls=%fused_computation.35 | convolution fusion | flops 1815085056 | bytes 9832448 | tf_op jit(solution)/shard_map/dot_general | solution.py:39
  84.9 1.0 copy-done.7
  85.9 0.8 slice.45
  86.7 1.2 copy.27
  87.9 0.1 multiply_reduce_fusion.5
  88.0 0.8 mul.130
  88.8 1.9 copy.29
  90.7 0.8 sub.89
  91.5 1.9 copy.28
  93.5 1.0 fusion.49
  94.5 2.2 fusion.59
  96.7 0.8 pad_maximum_fusion.3
  97.5 25.5 %all-gather.8.cloned.1.call-done = bf16[3072,384]{1,0:T(8,128)(2,1)} async-done(((bf16[192,384]{1,0:T(8,128)(2,1)}), bf16[3072,384]{1,0:T(8,128)(2,1)}) %all-gather.8.cloned.1.call-update) | async-done | bytes 2359312 | tf_op jit(solution)/shard_map/all_gather | solution.py:35
  123.0 2.6 fusion.39
  125.7 0.8 copy.34
  126.5 1.2 copy.31
  127.7 0.1 multiply_reduce_fusion.4
  127.8 33.2 %all-gather.6.cloned.1.call-done = bf16[2,1024,384]{2,1,0:T(8,128)(2,1)} async-done(((bf16[2,256,384]{2,1,0:T(8,128)(2,1)}), bf16[2,1024,384]{2,1,0:T(8,128)(2,1)}) %all-gather.6.cloned.1.call-update) | async-done | bytes 1572880 | tf_op jit(solution)/shard_map/all_gather | solution.py:70
  161.0 2.7 fusion.58
  163.6 2.3 copy.30
  166.0 2.3 copy.35
  168.2 2.0 fusion.9
  170.3 1.7 fusion.27
  171.9 1.3 multiply_reduce_fusion.3
  173.3 1.1 multiply_convert_fusion
  174.4 1.2 copy-done.3
  175.6 1.3 convolution_convert_fusion.3
  176.9 2.3 copy.38
  179.2 2.3 copy.39
  181.5 2.7 pad_maximum_fusion.1
  184.2 0.2 all-reduce.2.cloned.1.call-start
  184.5 2.3 fusion.57
  186.8 0.8 multiply_convert_fusion.1
  187.6 1.7 copy.44
  189.3 29.4 %reduce-scatter.3.cloned.1.call-done = bf16[2,256,384]{2,1,0:T(8,128)(2,1)} async-done(((bf16[2,1024,384]{2,1,0:T(8,128)(2,1)}), bf16[2,256,384]{2,1,0:T(8,128)(2,1)}) %reduce-scatter.3.cloned.1.call-update) | async-done | bytes 393232 | tf_op jit(solution)/shard_map/reduce_scatter | solution.py:104
  218.7 1.9 slice_convert_fusion.1
  220.6 1.9 copy.40
  222.5 1.2 multiply_reduce_fusion.1
  223.7 0.8 mul.146
  224.5 1.9 copy.42
  226.4 0.8 sub.100
  227.2 1.9 copy.41
  229.1 1.6 fusion.46
  230.7 0.7 copy-done.8
  231.4 6.5 %convolution_convert_fusion.2 = bf16[256,3072]{1,0:T(8,128)(2,1)} fusion(bf16[3072,1152]{1,0:T(8,128)(2,1)} %all-gather.4.cloned.1.call-done, bf16[256,384]{1,0:T(8,128)(2,1)S(1)} %copy-done.13, bf16[256,384]{1,0:T(8,128)(2,1)S(1)} %fusion.46, bf16[256,384]{1,0:T(8,128)(2,1)S(1)} %copy-done.10), kind=kOutput, calls=%fused_computation.7 | convolution fusion | flops 1814495232 | bytes 9240576 | tf_op jit(solution)/shard_map/rc,dc->rd/dot_general | solution.py:117
  237.9 0.0 reduce-scatter.5.cloned.1.call-start
  238.0 3.5 fusion
  241.5 0.9 fusion.48
  242.4 2.2 copy.45
  244.5 5.5 %convolution_convert_fusion = bf16[3072,3,384]{2,0,1:T(8,128)(2,1)} fusion(bf16[3,384,256]{2,1,0:T(8,128)(2,1)} %bitcast.107, bf16[1,256,3072]{2,1,0:T(8,128)(2,1)S(1)} %copy-done.1, f32[256]{0:T(256)S(1)} %copy-done.17, f32[256]{0:T(256)S(1)} %copy-done.19), kind=kOutput, calls=%fused_computation.1 | convolution fusion | flops 1818624000 | bytes 9242624 | tf_op jit(solution)/shard_map/rd,rc->dc/dot_general | solution.py:129
  250.1 8.4 %pad_maximum_fusion = bf16[3072,4,384]{2,0,1:T(8,128)(2,1)} fusion(bf16[3072,1,384]{2,0,1:T(8,128)(2,1)} %fusion, bf16[3072,3,384]{2,0,1:T(8,128)(2,1)} %convolution_convert_fusion), kind=kLoop, calls=%fused_computation | loop fusion | flops 4718592 | bytes 18874368 | tf_op jit(solution)/shard_map/concatenate | solution.py:136
  258.5 29.9 %all-reduce.2.cloned.1.call-done = bf16[256,3072]{1,0:T(8,128)(2,1)} async-done(((bf16[256,3072]{1,0:T(8,128)(2,1)}), bf16[256,3072]{1,0:T(8,128)(2,1)}) %all-reduce.2.cloned.1.call-update) | async-done | bytes 1572880 | tf_op jit(solution)/shard_map/psum | solution.py:120
  288.4 1.9 convert_element_type.80
  290.3 1.1 convert_reduce_fusion.1
  291.4 1.2 fusion.43
  292.6 111.0 %reduce-scatter.5.cloned.1.call-done = bf16[192,4,384]{2,0,1:T(8,128)(2,1)} async-done(((bf16[3072,4,384]{2,0,1:T(8,128)(2,1)}), bf16[192,4,384]{2,0,1:T(8,128)(2,1)}) %reduce-scatter.5.cloned.1.call-update) | async-done | bytes 589840 | tf_op jit(solution)/shard_map/reduce_scatter | solution.py:135
  403.6 1.2 convert_element_type.78
  404.9 0.7 slice_bitcast_fusion
  405.6 1.0 slice.52
  (58 shorter events, 0.5 us)
Async XLA Ops:
  7.2 115.9 %copy-start = (bf16[1,256,3072]{2,1,0:T(8,128)(2,1)S(1)}, bf16[1,256,3072]{2,1,0:T(8,128)(2,1)}, u32[]{:S(2)}) copy-start(bf16[1,256,3072]{2,1,0:T(8,128)(2,1)} %param.5) | copy-start | bytes 4718596
  7.2 4.6 %copy-start.1 = (bf16[1,256,3072]{2,1,0:T(8,128)(2,1)S(1)}, bf16[1,256,3072]{2,1,0:T(8,128)(2,1)}, u32[]{:S(2)}) copy-start(bf16[1,256,3072]{2,1,0:T(8,128)(2,1)} %param.4) | copy-start | bytes 4718596
  7.2 72.5 %all-gather.4.cloned.1.call-start = ((), (), s32[]{:S(2)}) async-start(), calls=%async_computation.2 | async-start | bytes 7520256 | tf_op jit(solution)/shard_map/all_gather | solution.py:34
  9.2 113.8 %all-gather.8.cloned.1.call-start = ((), (), s32[]{:S(2)}) async-start(), calls=%async_computation.4 | async-start | bytes 2506752 | tf_op jit(solution)/shard_map/all_gather | solution.py:35
  10.0 151.0 %all-gather.6.cloned.1.call-start = ((), (), s32[]{:S(2)}) async-start(), calls=%async_computation.3 | async-start | bytes 1966080 | tf_op jit(solution)/shard_map/all_gather | solution.py:70
  11.7 73.2 %copy-start.18 = (f32[256]{0:T(256)}, f32[256]{0:T(256)S(1)}, u32[]{:S(2)}) copy-start(f32[256]{0:T(256)S(1)} %broadcast_multiply_fusion.8) | copy-start | bytes 3076
  12.3 72.6 %copy-start.16 = (f32[256]{0:T(256)}, f32[256]{0:T(256)S(1)}, u32[]{:S(2)}) copy-start(f32[256]{0:T(256)S(1)} %add_rsqrt_fusion.2) | copy-start | bytes 3076
  84.9 1.0 copy-start.7
  87.9 8.8 %copy-start.2 = (f32[256,384]{0,1:T(8,128)}, f32[256,384]{0,1:T(8,128)S(1)}, u32[]{:S(2)}) copy-start(f32[256,384]{0,1:T(8,128)S(1)} %copy.27) | copy-start | bytes 1179652
  97.5 121.2 %reduce-scatter.3.cloned.1.call-start = ((), (), s32[]{:S(2)}) async-start(), calls=%async_computation.5 | async-start | bytes 1966080 | tf_op jit(solution)/shard_map/reduce_scatter | solution.py:104
  168.2 2.0 copy-start.15
  170.2 1.7 copy-start.12
  174.4 1.2 copy-start.3
  184.2 104.2 %all-reduce.2.cloned.1.call-start = ((), (), s32[]{:S(2)}) async-start(), calls=%async_computation.7 | async-start | bytes 3145728 | tf_op jit(solution)/shard_map/psum | solution.py:120
  189.3 39.8 %copy-start.6 = (f32[256,384]{1,0:T(8,128)S(1)}, f32[256,384]{1,0:T(8,128)}, u32[]{:S(2)}) copy-start(f32[256,384]{1,0:T(8,128)} %copy.29) | copy-start | bytes 1179652
  229.1 2.3 copy-start.10
  229.1 2.3 copy-start.13
  230.7 0.7 copy-start.8
  237.9 3.6 copy-start.9
  237.9 3.6 copy-start.11
  237.9 165.7 %reduce-scatter.5.cloned.1.call-start = ((), (), s32[]{:S(2)}) async-start(), calls=%async_computation.6 | async-start | bytes 10027008 | tf_op jit(solution)/shard_map/reduce_scatter | solution.py:135
  238.0 3.6 copy-start.14
  238.0 6.6 %copy-start.17 = (f32[256]{0:T(256)S(1)}, f32[256]{0:T(256)}, u32[]{:S(2)}) copy-start(f32[256]{0:T(256)} %copy-done.16) | copy-start | bytes 3076
  238.0 6.6 %copy-start.19 = (f32[256]{0:T(256)S(1)}, f32[256]{0:T(256)}, u32[]{:S(2)}) copy-start(f32[256]{0:T(256)} %copy-done.18) | copy-start | bytes 3076
  288.4 1.9 copy-start.4
  403.6 2.0 copy-start.5
Sparse Core Ops, SparseCore 0:
  10.9 68.7 all-gather.3
  81.9 41.0 all-gather.7
  125.2 35.7 all-gather.5
  184.4 34.2 reduce-scatter.2
  238.0 50.3 all-reduce.1
  292.4 111.2 reduce-scatter.4
where the time goes:
time: 415 us; the launch traced here: 413 us
  waiting for transfers between devices  297 us (72%)
  local copies, waits for them, and re-layouts  40.1 us (10%)
  matrix products  33.2 us (8%)
  other arithmetic  28.3 us (7%)
  between operations  14.4 us (3%)
    reduce_scatter x1, waiting for transfers between devices, local(): lax.psum_scatter(jnp.concatenate([qkv_term, out_term[:, None, :]], axis=1...  111 us
    all_gather x1, waiting for transfers between devices, local(): piece_qkv = lax.all_gather(flat_weight, ('seq', 'dp'), axis=0, tiled=True)  67.3 us
    all_gather x1, waiting for transfers between devices, local(): every_pair = lax.all_gather(key_value, 'seq', axis=1, tiled=True)  33.2 us
    psum x1, waiting for transfers between devices, local(): lax.psum(inner_grad.astype(jnp.bfloat16), 'tensor').astype(jnp.float32)  29.9 us
    reduce_scatter x1, waiting for transfers between devices, local(): lax.psum_scatter(every_grad.astype(jnp.bfloat16), 'seq', scatter_dimensio...  29.4 us
    all_gather x1, waiting for transfers between devices, local(): piece_out = lax.all_gather(out_weight, ('seq', 'dp'), axis=0, tiled=True)  25.5 us
    concatenate x1, other arithmetic, local(): jnp.concatenate([qkv_term, out_term[:, None, :]], axis=1)  8.4 us
  transfers between devices with their start and end apart: 6, of which 6 were waited for; matrix products, arithmetic and copies ran while one was open for 13% of the time, Pallas kernels for 0%

commit v1 on v0

--- a/solution.py
+++ b/solution.py
@@ -67,7 +67,12 @@
             * score_scale
         )
 
-    every_pair = lax.all_gather(key_value, "seq", axis=1, tiled=True)
+    ring = [key_value]
+    for hop in range(3):
+        ring.append(lax.ppermute(ring[-1], "seq", [(dev, (dev + 1) % 4) for dev in range(4)]))
+    every_pair = jnp.roll(
+        jnp.concatenate(ring[::-1], axis=1), (lax.axis_index("seq") + 1) * ring[0].shape[1], axis=1
+    )
     piece_rows = every_pair.shape[1]
     exponent = jnp.exp(scores_of(every_pair[0]))
     add_exp_total = jnp.sum(exponent, axis=-1)

time: 415 us -> 402 us (0.969)
  waiting for transfers between devices: 297 us -> 276 us
  starting transfers between devices: 0.42 us -> 4.63 us
    all_gather x1 -> x0, waiting for transfers between devices: 33.2 us -> none  [local(): every_pair = lax.all_gather(key_value, 'seq', axis=1, tiled=True)]
    ppermute x0 -> x3, waiting for transfers between devices: none -> 23.7 us  [local(): lax.ppermute(ring[-1], 'seq', [(dev, (dev + 1) % 4) for dev in range(4)])]
    all_gather x1, waiting for transfers between devices: 25.5 us -> 15.4 us  [local(): piece_out = lax.all_gather(out_weight, ('seq', 'dp'), axis=0, tiled=True)]
    unnamed x40 -> x48, local copies, waits for them, and re-layouts: 2.96 us -> 7.29 us
    ppermute x0 -> x3, starting transfers between devices: none -> 4.25 us  [local(): lax.ppermute(ring[-1], 'seq', [(dev, (dev + 1) % 4) for dev in range(4)])]
  transfers between devices with their start and end apart: 6 -> 8, of which waited for: 6 -> 7; matrix products, arithmetic and copies ran while one was open for 13% -> 13% of each run, Pallas kernels for 0% -> 0%
where the time goes in v1:
time: 402 us; the launch traced here: 401 us
  waiting for transfers between devices  276 us (69%)
  local copies, waits for them, and re-layouts  44.1 us (11%)
  matrix products  33.4 us (8%)
  other arithmetic  28.7 us (7%)
  between operations  14.1 us (4%)
  starting transfers between devices  4.63 us (1%)
    reduce_scatter x1, waiting for transfers between devices, local(): lax.psum_scatter(jnp.concatenate([qkv_term, out_term[:, None, :]], axis=1...  111 us
    all_gather x1, waiting for transfers between devices, local(): piece_qkv = lax.all_gather(flat_weight, ('seq', 'dp'), axis=0, tiled=True)  67.3 us
    psum x1, waiting for transfers between devices, local(): lax.psum(inner_grad.astype(jnp.bfloat16), 'tensor').astype(jnp.float32)  29.9 us
    reduce_scatter x1, waiting for transfers between devices, local(): lax.psum_scatter(every_grad.astype(jnp.bfloat16), 'seq', scatter_dimensio...  28 us
    ppermute x3, waiting for transfers between devices, local(): lax.ppermute(ring[-1], 'seq', [(dev, (dev + 1) % 4) for dev in range(4)])  23.7 us
    all_gather x1, waiting for transfers between devices, local(): piece_out = lax.all_gather(out_weight, ('seq', 'dp'), axis=0, tiled=True)  15.4 us
    concatenate x1, other arithmetic, local(): jnp.concatenate([qkv_term, out_term[:, None, :]], axis=1)  8.4 us
  transfers between devices with their start and end apart: 8, of which 7 were waited for; matrix products, arithmetic and copies ran while one was open for 13% of the time, Pallas kernels for 0%

profile of v1, /device:TPU:0, one launch (start us, length us, event | category | flops | bytes accessed | tf_op | source)
XLA Modules:
  0.0 400.9 jit_solution(12701628026478769434)
XLA Ops:
  7.2 2.0 copy.55
  10.0 1.7 convert_reduce_fusion
  12.3 67.3 %all-gather.3.cloned.1.call-done = bf16[3072,1152]{1,0:T(8,128)(2,1)} async-done(((bf16[192,1152]{1,0:T(8,128)(2,1)}), bf16[3072,1152]{1,0:T(8,128)(2,1)}) %all-gather.3.cloned.1.call-update) | async-done | bytes 7077904 | tf_op jit(solution)/shard_map/all_gather | solution.py:34
  79.6 5.3 %fusion.23 = f32[256,1152]{1,0:T(8,128)S(1)} fusion(bf16[3072,1152]{1,0:T(8,128)(2,1)} %all-gather.3.cloned.1.call-done, bf16[1,256,3072]{2,1,0:T(8,128)(2,1)S(1)} %copy-done.1, f32[256]{0:T(256)S(1)} %add_rsqrt_fusion.2, f32[256]{0:T(256)S(1)} %broadcast_multiply_fusion.8), kind=kOutput, calls=%fused_computation.35 | convolution fusion | flops 1815085056 | bytes 9832448 | tf_op jit(solution)/shard_map/dot_general | solution.py:39
  84.9 1.0 copy-done.10
  85.9 0.8 slice.45
  86.7 1.2 copy.27
  88.0 0.8 mul.133
  88.8 1.9 copy.29
  90.7 0.8 sub.93
  91.5 1.9 copy.28
  93.4 1.0 fusion.49
  94.5 2.2 fusion.58
  96.8 1.6 collective-permute-start
  98.4 11.8 %collective-permute-done = bf16[2,256,384]{2,1,0:T(8,128)(2,1)} collective-permute-done((bf16[2,256,384]{2,1,0:T(8,128)(2,1)S(1)}, bf16[2,256,384]{2,1,0:T(8,128)(2,1)}, u32[]{:S(2)}, u32[]{:S(2)}) %collective-permute-start) | collective-permute-done | bytes 393248 | tf_op jit(solution)/shard_map/ppermute | solution.py:72
  110.2 1.3 collective-permute-start.1
  111.5 15.4 %all-gather.5.cloned.1.call-done = bf16[3072,384]{1,0:T(8,128)(2,1)} async-done(((bf16[192,384]{1,0:T(8,128)(2,1)}), bf16[3072,384]{1,0:T(8,128)(2,1)}) %all-gather.5.cloned.1.call-update) | async-done | bytes 2359312 | tf_op jit(solution)/shard_map/all_gather | solution.py:35
  126.8 2.6 fusion.39
  129.5 0.8 copy.34
  130.3 1.2 copy.31
  131.5 1.4 collective-permute-start.2
  133.0 11.9 %collective-permute-done.2 = bf16[2,256,384]{2,1,0:T(8,128)(2,1)S(1)} collective-permute-done((bf16[2,256,384]{2,1,0:T(8,128)(2,1)}, bf16[2,256,384]{2,1,0:T(8,128)(2,1)S(1)}, u32[]{:S(2)}, u32[]{:S(2)}) %collective-permute-start.2) | collective-permute-done | bytes 393248 | tf_op jit(solution)/shard_map/ppermute | solution.py:72
  144.9 1.1 constant_dynamic-update-slice_fusion.6
  146.0 1.1 constant_dynamic-update-slice_fusion.5
  147.0 1.1 constant_dynamic-update-slice_fusion.4
  148.2 1.1 constant_dynamic-update-slice_fusion.2
  149.3 1.1 constant_dynamic-update-slice_fusion.1
  150.4 1.3 constant_dynamic-slice_fusion
  151.7 2.3 copy.30
  154.0 2.3 copy.35
  156.3 2.0 fusion.9
  158.3 1.7 fusion.27
  160.0 1.3 multiply_reduce_fusion.3
  161.3 1.1 multiply_convert_fusion
  162.4 1.2 copy-done.3
  163.6 1.3 convolution_convert_fusion.3
  164.9 2.3 copy.38
  167.2 2.3 copy.39
  169.5 2.7 pad_maximum_fusion.1
  172.5 2.3 fusion.57
  174.8 0.8 multiply_convert_fusion.1
  175.6 1.8 copy.44
  177.4 28.0 %reduce-scatter.3.cloned.1.call-done = bf16[2,256,384]{2,1,0:T(8,128)(2,1)} async-done(((bf16[2,1024,384]{2,1,0:T(8,128)(2,1)}), bf16[2,256,384]{2,1,0:T(8,128)(2,1)}) %reduce-scatter.3.cloned.1.call-update) | async-done | bytes 393232 | tf_op jit(solution)/shard_map/reduce_scatter | solution.py:109
  205.4 1.9 slice_convert_fusion.1
  207.3 1.9 copy.40
  209.2 1.2 multiply_reduce_fusion.1
  210.4 0.8 mul.150
  211.2 1.9 copy.42
  213.1 0.8 sub.105
  213.9 1.9 copy.41
  215.8 1.6 fusion.46
  218.0 6.7 %convolution_convert_fusion.2 = bf16[256,3072]{1,0:T(8,128)(2,1)} fusion(bf16[3072,1152]{1,0:T(8,128)(2,1)} %all-gather.3.cloned.1.call-done, bf16[256,384]{1,0:T(8,128)(2,1)} %get-tuple-element.15, bf16[256,384]{1,0:T(8,128)(2,1)S(1)} %fusion.46, bf16[256,384]{1,0:T(8,128)(2,1)} %copy.44), kind=kOutput, calls=%fused_computation.7 | convolution fusion | flops 1814495232 | bytes 9240576 | tf_op jit(solution)/shard_map/rc,dc->rd/dot_general | solution.py:122
  224.8 3.5 fusion
  228.4 0.9 fusion.48
  229.3 2.2 copy.45
  231.4 5.5 %convolution_convert_fusion = bf16[3072,3,384]{2,0,1:T(8,128)(2,1)} fusion(bf16[3,384,256]{2,1,0:T(8,128)(2,1)} %bitcast.107, bf16[1,256,3072]{2,1,0:T(8,128)(2,1)S(1)} %copy-done.1, f32[256]{0:T(256)S(1)} %copy-done.18, f32[256]{0:T(256)S(1)} %copy-done.20), kind=kOutput, calls=%fused_computation.1 | convolution fusion | flops 1818624000 | bytes 9242624 | tf_op jit(solution)/shard_map/rd,rc->dc/dot_general | solution.py:134
  237.0 8.4 %pad_maximum_fusion = bf16[3072,4,384]{2,0,1:T(8,128)(2,1)} fusion(bf16[3072,1,384]{2,0,1:T(8,128)(2,1)} %fusion, bf16[3072,3,384]{2,0,1:T(8,128)(2,1)} %convolution_convert_fusion), kind=kLoop, calls=%fused_computation | loop fusion | flops 4718592 | bytes 18874368 | tf_op jit(solution)/shard_map/concatenate | solution.py:141
  245.4 29.9 %all-reduce.2.cloned.1.call-done = bf16[256,3072]{1,0:T(8,128)(2,1)} async-done(((bf16[256,3072]{1,0:T(8,128)(2,1)}), bf16[256,3072]{1,0:T(8,128)(2,1)}) %all-reduce.2.cloned.1.call-update) | async-done | bytes 1572880 | tf_op jit(solution)/shard_map/psum | solution.py:125
  275.3 1.9 convert_element_type.80
  277.2 1.1 convert_reduce_fusion.1
  278.3 1.2 fusion.43
  279.5 111.0 %reduce-scatter.5.cloned.1.call-done = bf16[192,4,384]{2,0,1:T(8,128)(2,1)} async-done(((bf16[3072,4,384]{2,0,1:T(8,128)(2,1)}), bf16[192,4,384]{2,0,1:T(8,128)(2,1)}) %reduce-scatter.5.cloned.1.call-update) | async-done | bytes 589840 | tf_op jit(solution)/shard_map/reduce_scatter | solution.py:140
  390.5 1.1 convert_element_type.78
  392.4 2.0 slice.50
  (71 shorter events, 3.7 us)
Async XLA Ops:
  7.2 119.7 %copy-start = (bf16[1,256,3072]{2,1,0:T(8,128)(2,1)S(1)}, bf16[1,256,3072]{2,1,0:T(8,128)(2,1)}, u32[]{:S(2)}) copy-start(bf16[1,256,3072]{2,1,0:T(8,128)(2,1)} %param.5) | copy-start | bytes 4718596
  7.2 4.6 %copy-start.1 = (bf16[1,256,3072]{2,1,0:T(8,128)(2,1)S(1)}, bf16[1,256,3072]{2,1,0:T(8,128)(2,1)}, u32[]{:S(2)}) copy-start(bf16[1,256,3072]{2,1,0:T(8,128)(2,1)} %param.4) | copy-start | bytes 4718596
  7.2 72.5 %all-gather.3.cloned.1.call-start = ((), (), s32[]{:S(2)}) async-start(), calls=%async_computation.2 | async-start | bytes 7520256 | tf_op jit(solution)/shard_map/all_gather | solution.py:34
  9.2 117.6 %all-gather.5.cloned.1.call-start = ((), (), s32[]{:S(2)}) async-start(), calls=%async_computation.3 | async-start | bytes 2506752 | tf_op jit(solution)/shard_map/all_gather | solution.py:35
  10.0 195.4 %reduce-scatter.3.cloned.1.call-start = ((), (), s32[]{:S(2)}) async-start(), calls=%async_computation.4 | async-start | bytes 1966080 | tf_op jit(solution)/shard_map/reduce_scatter | solution.py:109
  11.7 73.2 %copy-start.19 = (f32[256]{0:T(256)}, f32[256]{0:T(256)S(1)}, u32[]{:S(2)}) copy-start(f32[256]{0:T(256)S(1)} %broadcast_multiply_fusion.8) | copy-start | bytes 3076
  12.3 72.6 %copy-start.17 = (f32[256]{0:T(256)}, f32[256]{0:T(256)S(1)}, u32[]{:S(2)}) copy-start(f32[256]{0:T(256)S(1)} %add_rsqrt_fusion.2) | copy-start | bytes 3076
  84.9 1.0 copy-start.10
  87.9 8.9 %copy-start.2 = (f32[256,384]{0,1:T(8,128)}, f32[256,384]{0,1:T(8,128)S(1)}, u32[]{:S(2)}) copy-start(f32[256,384]{0,1:T(8,128)S(1)} %copy.27) | copy-start | bytes 1179652
  94.5 15.7 %copy-start.8 = (bf16[1,256,384]{2,1,0:T(8,128)(2,1)}, bf16[1,256,384]{2,1,0:T(8,128)(2,1)S(1)}, u32[]{:S(2)}) copy-start(bf16[1,256,384]{2,1,0:T(8,128)(2,1)S(1)} %fusion.49) | copy-start | bytes 589828
  96.7 1.6 copy-start.6
  96.8 13.4 %collective-permute-start = (bf16[2,256,384]{2,1,0:T(8,128)(2,1)S(1)}, bf16[2,256,384]{2,1,0:T(8,128)(2,1)}, u32[]{:S(2)}, u32[]{:S(2)}) collective-permute-start(bf16[2,256,384]{2,1,0:T(8,128)(2,1)S(1)} %pad_maximum_fusion.3), channel_id=1, source_target_pairs={{0,8},{8,16},{16,24},{24,0},{1,9},{9,17},{17,25},{25,1},{2,10},{10... | collective-permute-start | bytes 1179656 | tf_op jit(solution)/shard_map/ppermute | solution.py:72
  110.2 21.4 %collective-permute-start.1 = (bf16[2,256,384]{2,1,0:T(8,128)(2,1)}, bf16[2,256,384]{2,1,0:T(8,128)(2,1)}, u32[]{:S(2)}, u32[]{:S(2)}) collective-permute-start(bf16[2,256,384]{2,1,0:T(8,128)(2,1)} %collective-permute-done), channel_id=1, source_target_pairs={{0,8},{8,16},{16,24},{24,0},{1,9},{9,17},{17,25},{25,1},{2,10},{10... | collective-permute-start | bytes 1179656 | tf_op jit(solution)/shard_map/ppermute | solution.py:72
  131.5 18.8 %copy-start.7 = (bf16[1,256,384]{2,1,0:T(8,128)(2,1)S(1)}, bf16[1,256,384]{2,1,0:T(8,128)(2,1)}, u32[]{:S(2)}) copy-start(bf16[1,256,384]{2,1,0:T(8,128)(2,1)} %copy-done.6) | copy-start | bytes 589828
  131.5 18.8 %copy-start.9 = (bf16[1,256,384]{2,1,0:T(8,128)(2,1)S(1)}, bf16[1,256,384]{2,1,0:T(8,128)(2,1)}, u32[]{:S(2)}) copy-start(bf16[1,256,384]{2,1,0:T(8,128)(2,1)} %copy-done.8) | copy-start | bytes 589828
  131.5 13.3 %collective-permute-start.2 = (bf16[2,256,384]{2,1,0:T(8,128)(2,1)}, bf16[2,256,384]{2,1,0:T(8,128)(2,1)S(1)}, u32[]{:S(2)}, u32[]{:S(2)}) collective-permute-start(bf16[2,256,384]{2,1,0:T(8,128)(2,1)} %collective-permute-done.1), channel_id=1, source_target_pairs={{0,8},{8,16},{16,24},{24,0},{1,9},{9,17},{17,25},{25,1},{2,10},{10... | collective-permute-start | bytes 1179656 | tf_op jit(solution)/shard_map/ppermute | solution.py:72
  156.3 2.0 copy-start.16
  158.3 1.7 copy-start.14
  162.4 1.2 copy-start.3
  172.3 103.0 %all-reduce.2.cloned.1.call-start = ((), (), s32[]{:S(2)}) async-start(), calls=%async_computation.6 | async-start | bytes 3145728 | tf_op jit(solution)/shard_map/psum | solution.py:125
  175.6 40.2 %copy-start.5 = (f32[256,384]{1,0:T(8,128)S(1)}, f32[256,384]{1,0:T(8,128)}, u32[]{:S(2)}) copy-start(f32[256,384]{1,0:T(8,128)} %copy.29) | copy-start | bytes 1179652
  217.4 0.7 copy-start.11
  224.7 3.6 copy-start.12
  224.7 3.6 copy-start.13
  224.8 165.7 %reduce-scatter.5.cloned.1.call-start = ((), (), s32[]{:S(2)}) async-start(), calls=%async_computation.5 | async-start | bytes 10027008 | tf_op jit(solution)/shard_map/reduce_scatter | solution.py:140
  224.8 3.6 copy-start.15
  224.8 6.6 %copy-start.18 = (f32[256]{0:T(256)S(1)}, f32[256]{0:T(256)}, u32[]{:S(2)}) copy-start(f32[256]{0:T(256)} %copy-done.17) | copy-start | bytes 3076
  224.8 6.6 %copy-start.20 = (f32[256]{0:T(256)S(1)}, f32[256]{0:T(256)}, u32[]{:S(2)}) copy-start(f32[256]{0:T(256)} %copy-done.19) | copy-start | bytes 3076
  275.3 1.9 copy-start.4
Sparse Core Ops, SparseCore 0:
  10.9 68.7 all-gather.2
  81.9 44.8 all-gather.4
  172.4 32.9 reduce-scatter.2
  224.9 50.3 all-reduce.1
  279.2 111.2 reduce-scatter.4
